TPU v7x, 256 devices: a whole 4x4x8 slice. The times are simulated.
256 devices in a mesh: dp: 32 (over y, x, core), seq: 8 (over z).
Axes of the slice: x: 4, y: 4, z: 8, core: 2. Of those that a mesh axis runs over, the one named last changes fastest.
Arguments:
- query_rows: bfloat16 [32, 1024, 3072], P('dp', 'seq'), may hold values from -6 to 6
- key_rows: bfloat16 [32, 1024, 3072], P('dp', 'seq'), may hold values from -6 to 6
- value_rows: bfloat16 [32, 1024, 3072], P('dp', 'seq'), may hold values from -6 to 6
- out_grad: bfloat16 [32, 1024, 6144], P('dp', 'seq'), may hold values from -54 to 54
- clip_lengths: int32 [32, 4], P('dp'), may hold values from 1 to 512, 1024 in all within a row
- out_weight: bfloat16 [3072, 6144], P('seq'), may hold values from -0.109375 to 0.109375
- query_gain: float32 [128], replicated, may hold values from 0.1 to 1.9
- key_gain: float32 [128], replicated, may hold values from 0.1 to 1.9
Outputs:
- query_grad: bfloat16 [32, 1024, 3072], P('dp', 'seq')
- key_grad: bfloat16 [32, 1024, 3072], P('dp', 'seq')
- value_grad: bfloat16 [32, 1024, 3072], P('dp', 'seq')
- weight_grad: float32 [3072, 6144], P('seq', 'dp')
- querygain_grad: float32 [128], replicated
- keygain_grad: float32 [128], replicated
- grad_norm: float32 [], replicated
Inputs may be any that keep to these rules, and one draw needn't show every extreme that they name: `clip_lengths`: the token counts of each group's clips sum to 1024.
All inputs are finite; a program needn't handle non-finite values.
Results may differ from a plain program's by a relative error of at most 0.015.
Values may be sent and summed in bfloat16 or wider, within the bound.
A program may use at most 128 MiB of HBM per device.

v0:
```python
import jax
import jax.numpy as jnp
from jax import lax
from jax.sharding import Mesh
from jax.sharding import PartitionSpec as P

HEAD_DIM = 128
MAX_NORM = 768
DP = ("dp_0", "dp_1", "dp_2")
DP_SEQ = ("dp_0", "dp_1", "dp_2", "seq")
EPS = 1e-06


def one_axis_at_a_time(array, axes):
    for axis in axes:
        array = lax.psum(array, axis)
    return array


def segment_ids(lengths, total):
    ends = jnp.cumsum(lengths)
    places = jnp.arange(total, dtype=jnp.int32)
    return jnp.sum((places[:, None] >= ends[None, :]).astype(jnp.int32), axis=1)


def norm_rows(rows, gain):
    wide = rows.astype(jnp.float32)
    inverse = lax.rsqrt(jnp.mean(wide * wide, axis=-1, keepdims=True) + EPS)
    unit = wide * inverse
    return (unit, inverse, (unit * gain).astype(jnp.bfloat16))


def norm_back(unit, inverse, gain, d_norm):
    gain_part = jnp.sum(unit * d_norm, axis=(0, 1))
    d_unit = d_norm * gain
    d_rows = inverse * (d_unit - unit * jnp.mean(unit * d_unit, axis=-1, keepdims=True))
    return (d_rows.astype(jnp.bfloat16), gain_part)


def local(
    query_rows, key_rows, value_rows, out_grad, clip_lengths, out_weight, query_gain, key_gain
):
    query, keys, values = (
        lax.all_to_all(query_rows[0], "seq", split_axis=1, concat_axis=0, tiled=True),
        lax.all_to_all(key_rows[0], "seq", split_axis=1, concat_axis=0, tiled=True),
        lax.all_to_all(value_rows[0], "seq", split_axis=1, concat_axis=0, tiled=True),
    )
    total = query.shape[0]
    heads = query.shape[1] // HEAD_DIM
    width = heads * HEAD_DIM
    scale = HEAD_DIM ** (-0.5)
    block = min(512, total)
    blocks = total // block
    seg = segment_ids(clip_lengths[0], total)
    q_unit, q_inv, q_norm = norm_rows(query.reshape(total, heads, HEAD_DIM), query_gain)
    k_unit, k_inv, k_norm = norm_rows(keys.reshape(total, heads, HEAD_DIM), key_gain)
    values3 = values.reshape(total, heads, HEAD_DIM)

    def forward_block(index):
        start = index * block
        query_block = lax.dynamic_slice_in_dim(q_norm, start, block, 0)
        seg_block = lax.dynamic_slice_in_dim(seg, start, block, 0)
        scores = (
            jnp.einsum("qhd,khd->hqk", query_block, k_norm, preferred_element_type=jnp.float32)
            * scale
        )
        same = seg_block[:, None] == seg[None, :]
        expo = jnp.where(same[None], jnp.exp(scores), 0.0)
        probs = (expo / jnp.sum(expo, axis=-1, keepdims=True)).astype(jnp.bfloat16)
        attn_out = jnp.einsum("hqk,khd->qhd", probs, values3, preferred_element_type=jnp.float32)
        return (probs, attn_out.astype(jnp.bfloat16))

    probs_all, attn_blocks = lax.map(forward_block, jnp.arange(blocks, dtype=jnp.int32))
    attn_flat = attn_blocks.reshape(total, width)
    out_full = lax.all_gather(out_grad[0], "seq", axis=0, tiled=True)
    weight_part = jnp.dot(attn_flat.T, out_full, preferred_element_type=jnp.float32)
    d_attn = jnp.dot(out_full, out_weight.T, preferred_element_type=jnp.float32).astype(
        jnp.bfloat16
    )
    d_attn3 = d_attn.reshape(total, heads, HEAD_DIM)

    def backward_block(carry, items):
        d_key, d_value = carry
        probs, index = items
        start = index * block
        attn_grad = lax.dynamic_slice_in_dim(d_attn3, start, block, 0)
        query_block = lax.dynamic_slice_in_dim(q_norm, start, block, 0)
        d_probs = jnp.einsum("qhd,khd->hqk", attn_grad, values3, preferred_element_type=jnp.float32)
        probs32 = probs.astype(jnp.float32)
        row_sum = jnp.sum(probs32 * d_probs, axis=-1, keepdims=True)
        d_scores = (probs32 * (d_probs - row_sum) * scale).astype(jnp.bfloat16)
        d_value = d_value + jnp.einsum(
            "hqk,qhd->khd", probs, attn_grad, preferred_element_type=jnp.float32
        )
        d_key = d_key + jnp.einsum(
            "hqk,qhd->khd", d_scores, query_block, preferred_element_type=jnp.float32
        )
        d_query = jnp.einsum("hqk,khd->qhd", d_scores, k_norm, preferred_element_type=jnp.float32)
        return ((d_key, d_value), d_query)

    empty = jnp.zeros((total, heads, HEAD_DIM), jnp.float32)
    (d_knorm, d_value32), d_query_blocks = lax.scan(
        backward_block, (empty, empty), (probs_all, jnp.arange(blocks, dtype=jnp.int32))
    )
    d_qnorm = d_query_blocks.reshape(total, heads, HEAD_DIM)
    query_grad, q_gain_part = norm_back(q_unit, q_inv, query_gain, d_qnorm)
    key_grad, k_gain_part = norm_back(k_unit, k_inv, key_gain, d_knorm)
    value_grad = d_value32.astype(jnp.bfloat16)
    query_back, key_back, value_back = (
        lax.all_to_all(
            query_grad.reshape(total, width), "seq", split_axis=0, concat_axis=1, tiled=True
        ),
        lax.all_to_all(
            key_grad.reshape(total, width), "seq", split_axis=0, concat_axis=1, tiled=True
        ),
        lax.all_to_all(
            value_grad.reshape(total, width), "seq", split_axis=0, concat_axis=1, tiled=True
        ),
    )
    weight_shard = lax.psum_scatter(
        weight_part.astype(jnp.bfloat16), DP, scatter_dimension=1, tiled=True
    ).astype(jnp.float32)
    local_squares = jnp.sum(weight_shard * weight_shard)
    qgain_raw, kgain_raw = (
        one_axis_at_a_time(q_gain_part, DP_SEQ),
        one_axis_at_a_time(k_gain_part, DP_SEQ),
    )
    weight_squares = one_axis_at_a_time(local_squares, DP_SEQ)
    squares = weight_squares + jnp.sum(qgain_raw * qgain_raw) + jnp.sum(kgain_raw * kgain_raw)
    grad_norm = jnp.sqrt(squares)
    factor = jnp.minimum(jnp.float32(1.0), MAX_NORM / (grad_norm + EPS))
    return (
        query_back[None],
        key_back[None],
        value_back[None],
        weight_shard * factor,
        qgain_raw * factor,
        kgain_raw * factor,
        grad_norm,
    )


def solution(mesh):
    torus = Mesh(mesh.devices.reshape(4, 4, 2, mesh.shape["seq"]), ("dp_0", "dp_1", "dp_2", "seq"))
    return jax.shard_map(
        local,
        mesh=torus,
        in_specs=(
            P(DP, "seq", None),
            P(DP, "seq", None),
            P(DP, "seq", None),
            P(DP, "seq", None),
            P(DP, None),
            P("seq", None),
            P(),
            P(),
        ),
        out_specs=(
            P(DP, "seq", None),
            P(DP, "seq", None),
            P(DP, "seq", None),
            P("seq", DP),
            P(),
            P(),
            P(),
        ),
        check_vma=False,
    )
```

profile of v0, /device:TPU:32, one launch (start us, length us, event | category | flops | bytes accessed | tf_op | source)
XLA Modules:
  0.0 430.5 jit_solution(6281215837916845542)
XLA Ops:
  9.5 8.6 %all-to-all-start = ((bf16[128,8,384]{0,2,1:T(8,128)(2,1)}), bf16[128,8,384]{0,2,1:T(8,128)(2,1)S(1)}, u32[]{:S(2)}, u32[]{:S(2)}) async-start(bf16[128,8,384]{0,2,1:T(8,128)(2,1)} %bitcast.4), calls=%async_computation | async-start | bytes 1572864 | tf_op jit(solution)/shard_map/all_to_all | solution.py:44
  19.2 26.2 %all-to-all-done = bf16[128,8,384]{0,2,1:T(8,128)(2,1)S(1)} async-done(((bf16[128,8,384]{0,2,1:T(8,128)(2,1)}), bf16[128,8,384]{0,2,1:T(8,128)(2,1)S(1)}, u32[]{:S(2)}, u32[]{:S(2)}) %all-to-all-start) | async-done | bytes 786464 | tf_op jit(solution)/shard_map/all_to_all | solution.py:44
  45.4 5.8 %all-to-all-start.1 = ((bf16[128,8,384]{0,2,1:T(8,128)(2,1)}), bf16[128,8,384]{0,2,1:T(8,128)(2,1)S(1)}, u32[]{:S(2)}, u32[]{:S(2)}) async-start(bf16[128,8,384]{0,2,1:T(8,128)(2,1)} %bitcast.8), calls=%async_computation.1 | async-start | bytes 1572864 | tf_op jit(solution)/shard_map/all_to_all | solution.py:45
  52.3 30.0 %all-to-all-done.1 = bf16[128,8,384]{0,2,1:T(8,128)(2,1)S(1)} async-done(((bf16[128,8,384]{0,2,1:T(8,128)(2,1)}), bf16[128,8,384]{0,2,1:T(8,128)(2,1)S(1)}, u32[]{:S(2)}, u32[]{:S(2)}) %all-to-all-start.1) | async-done | bytes 786464 | tf_op jit(solution)/shard_map/all_to_all | solution.py:45
  82.4 5.3 %all-to-all-start.2 = ((bf16[128,8,384]{0,2,1:T(8,128)(2,1)}), bf16[128,8,384]{0,2,1:T(8,128)(2,1)}, u32[]{:S(2)}, u32[]{:S(2)}) async-start(bf16[128,8,384]{0,2,1:T(8,128)(2,1)} %bitcast.10), calls=%async_computation.2 | async-start | bytes 1572864 | tf_op jit(solution)/shard_map/all_to_all | solution.py:46
  92.0 2.1 copy.147
  97.4 2.3 copy.151
  99.7 19.1 %all-to-all-done.2 = bf16[128,8,384]{0,2,1:T(8,128)(2,1)} async-done(((bf16[128,8,384]{0,2,1:T(8,128)(2,1)}), bf16[128,8,384]{0,2,1:T(8,128)(2,1)}, u32[]{:S(2)}, u32[]{:S(2)}) %all-to-all-start.2) | async-done | bytes 786464 | tf_op jit(solution)/shard_map/all_to_all | solution.py:46
  118.7 2.5 copy.149
  121.2 2.2 reshape.177
  123.4 2.3 copy.152
  128.8 21.1 %while.27 = (s32[]{:T(128)}, bf16[2,3,512,1024]{3,2,1,0:T(8,128)(2,1)}, bf16[2,512,3,128]{3,1,2,0:T(8,128)(2,1)}, s32[2]{0:T(128)S(1)}, s32[1024]{0:T(1024)S(1)}...) while((s32[]{:T(128)}, ...), condition=%wide.region_6.7_spmd, body=%wide.region_4.6_spmd.sunk | while | flops 817035776 | bytes 85746000 | solution.py:73
  130.5 3.4 fusion.75
  141.1 3.4 fusion.75
  149.9 3.1 copy.167
  153.0 2.1 copy.180
  156.8 32.1 %all-gather.3.cloned.1.call-done = bf16[1,1024,6144]{2,1,0:T(8,128)(2,1)} async-done(((bf16[1,128,6144]{2,1,0:T(8,128)(2,1)}), bf16[1,1024,6144]{2,1,0:T(8,128)(2,1)}) %all-gather.3.cloned.1.call-update) | async-done | bytes 12582928 | tf_op jit(solution)/shard_map/all_gather | solution.py:75
  188.9 11.4 %fusion.42 = bf16[384,6144]{0,1:T(8,128)(2,1)} fusion(bf16[1024,384]{0,1:T(8,128)(2,1)} %bitcast.161, bf16[1,1024,6144]{2,1,0:T(8,128)(2,1)} %all-gather.3.cloned.1.call-done), kind=kOutput, calls=%fused_computation.45 | convolution fusion | flops 4834197504 | bytes 18087936 | tf_op jit(solution)/shard_map/dot_general | solution.py:76
  200.3 10.4 %fusion.48 = bf16[1024,384]{0,1:T(8,128)(2,1)} fusion(bf16[384,6144]{1,0:T(8,128)(2,1)} %param.17, bf16[1,1024,6144]{2,1,0:T(8,128)(2,1)} %all-gather.3.cloned.1.call-done), kind=kOutput, calls=%fused_computation.62 | convolution fusion | flops 4832231424 | bytes 18087936 | tf_op jit(solution)/shard_map/dot_general | solution.py:77
  210.8 57.7 %while.28 = (s32[]{:T(128)}, f32[1024,3,128]{0,2,1:T(8,128)}, f32[1024,3,128]{0,2,1:T(8,128)S(1)}, f32[2,512,3,128]{3,1,2,0:T(8,128)}, s32[2]{0:T(128)S(1)}, /*i...) while((s32[]{:T(128)}, f32[1024,3,128]{0,2,1:T(8,128)}, ...), condition=%wide.region_9.10_spmd.clone, body=%wide.region_7.9_spmd.clone.sunk | while | flops 1634210816 | bytes 57019604 | solution.py:102
  212.0 5.0 %fusion.83 = f32[3,512,1024]{2,1,0:T(8,128)} fusion(bf16[1024,3,128]{2,0,1:T(8,128)(2,1)} %get-tuple-element.549, bf16[1024,3,128]{0,2,1:T(8,128)(2,1)} %get-tuple-element.548, s32[]{:T(128)S(6)} %select_n.24), kind=kOutput, calls=%fused_computation.30.clone.1 | convolution fusion | flops 402653184 | bytes 7471108 | tf_op jit(solution)/shard_map/while/body/eval_jaxpr/qhd,khd->hqk/dot_general | solution.py:88
  217.0 10.2 %bitcast_add_fusion.4 = f32[1024,3,128]{0,2,1:T(8,128)} fusion(f32[1024,3,128]{0,2,1:T(8,128)} %get-tuple-element.528, f32[3,512,1024]{2,1,0:T(8,128)} %fusion.83, bf16[2,3,512,1024]{3,2,1,0:T(8,128)(2,1)} %get-tuple-element.547, s32[]{:T(128)} %get-tuple-element.527, pred[]{:T(512)S(6)} %compare.3, bf16[1024,3,128]{0,2,1:T(8,128)(2,1)} %get-tuple-element.546, ...), kind=kOutput, calls=%fused_computation.26.clone.1 | convolution fusion | flops 414452224 | bytes 22414340 | tf_op jit(solution)/shard_map/while/body/eval_jaxpr/hqk,qhd->khd/dot_general | solution.py:95
  227.2 9.7 %fusion.84 = f32[2,512,3,128]{3,1,2,0:T(8,128)} fusion(f32[2,512,3,128]{3,1,2,0:T(8,128)} %get-tuple-element.530, s32[]{:T(128)} %get-tuple-element.527, bf16[1024,3,128]{2,0,1:T(8,128)(2,1)} %get-tuple-element.550, f32[3,512,1024]{2,1,0:T(8,128)} %fusion.83, bf16[2,3,512,1024]{3,2,1,0:T(8,128)(2,1)} %get-tuple-element.547), kind=kOutput, calls=%fused_computation.28.clone.1 | convolution fusion | flops 413665792 | bytes 20448768 | tf_op jit(solution)/shard_map/while/body/eval_jaxpr/hqk,khd->qhd/dot_general | solution.py:98
  236.9 3.0 bitcast_add_fusion.5
  241.2 4.9 %fusion.83 = f32[3,512,1024]{2,1,0:T(8,128)} fusion(bf16[1024,3,128]{2,0,1:T(8,128)(2,1)} %get-tuple-element.549, bf16[1024,3,128]{0,2,1:T(8,128)(2,1)} %get-tuple-element.548, s32[]{:T(128)S(6)} %select_n.24), kind=kOutput, calls=%fused_computation.30.clone.1 | convolution fusion | flops 402653184 | bytes 7471108 | tf_op jit(solution)/shard_map/while/body/eval_jaxpr/qhd,khd->hqk/dot_general | solution.py:88
  246.1 10.1 %bitcast_add_fusion.4 = f32[1024,3,128]{0,2,1:T(8,128)} fusion(f32[1024,3,128]{0,2,1:T(8,128)} %get-tuple-element.528, f32[3,512,1024]{2,1,0:T(8,128)} %fusion.83, bf16[2,3,512,1024]{3,2,1,0:T(8,128)(2,1)} %get-tuple-element.547, s32[]{:T(128)} %get-tuple-element.527, pred[]{:T(512)S(6)} %compare.3, bf16[1024,3,128]{0,2,1:T(8,128)(2,1)} %get-tuple-element.546, ...), kind=kOutput, calls=%fused_computation.26.clone.1 | convolution fusion | flops 414452224 | bytes 22414340 | tf_op jit(solution)/shard_map/while/body/eval_jaxpr/hqk,qhd->khd/dot_general | solution.py:95
  256.2 9.3 %fusion.84 = f32[2,512,3,128]{3,1,2,0:T(8,128)} fusion(f32[2,512,3,128]{3,1,2,0:T(8,128)} %get-tuple-element.530, s32[]{:T(128)} %get-tuple-element.527, bf16[1024,3,128]{2,0,1:T(8,128)(2,1)} %get-tuple-element.550, f32[3,512,1024]{2,1,0:T(8,128)} %fusion.83, bf16[2,3,512,1024]{3,2,1,0:T(8,128)(2,1)} %get-tuple-element.547), kind=kOutput, calls=%fused_computation.28.clone.1 | convolution fusion | flops 413665792 | bytes 20448768 | tf_op jit(solution)/shard_map/while/body/eval_jaxpr/hqk,khd->qhd/dot_general | solution.py:98
  265.5 2.9 bitcast_add_fusion.5
  268.5 3.7 copy.156
  272.2 2.7 copy.159
  274.9 3.0 copy.160
  277.9 2.3 multiply_reduce_fusion.3
  281.9 3.3 reshape.179
  285.3 4.3 fusion.47
  289.5 6.7 %all-to-all-start.3 = ((bf16[8,128,384]{1,2,0:T(8,128)(2,1)}), bf16[8,128,384]{1,2,0:T(8,128)(2,1)}, u32[]{:S(2)}, u32[]{:S(2)}) async-start(bf16[8,128,384]{1,2,0:T(8,128)(2,1)} %fusion.47), calls=%async_computation.3 | async-start | bytes 1572864 | tf_op jit(solution)/shard_map/all_to_all | solution.py:110
  296.2 2.0 multiply_reduce_fusion
  300.3 17.9 %all-to-all-done.3 = bf16[8,128,384]{1,2,0:T(8,128)(2,1)} async-done(((bf16[8,128,384]{1,2,0:T(8,128)(2,1)}), bf16[8,128,384]{1,2,0:T(8,128)(2,1)}, u32[]{:S(2)}, u32[]{:S(2)}) %all-to-all-start.3) | async-done | bytes 786464 | tf_op jit(solution)/shard_map/all_to_all | solution.py:110
  318.2 4.9 %all-to-all-start.4 = ((bf16[8,128,384]{2,1,0:T(8,128)(2,1)}), bf16[8,128,384]{2,1,0:T(8,128)(2,1)S(1)}, u32[]{:S(2)}, u32[]{:S(2)}) async-start(bf16[8,128,384]{2,1,0:T(8,128)(2,1)} %copy.163), calls=%async_computation.4 | async-start | bytes 1572864 | tf_op jit(solution)/shard_map/all_to_all | solution.py:113
  324.8 18.6 %all-to-all-done.4 = bf16[8,128,384]{2,1,0:T(8,128)(2,1)S(1)} async-done(((bf16[8,128,384]{2,1,0:T(8,128)(2,1)}), bf16[8,128,384]{2,1,0:T(8,128)(2,1)S(1)}, u32[]{:S(2)}, u32[]{:S(2)}) %all-to-all-start.4) | async-done | bytes 786464 | tf_op jit(solution)/shard_map/all_to_all | solution.py:113
  343.4 5.5 %all-to-all-start.5 = ((bf16[8,128,384]{2,1,0:T(8,128)(2,1)}), bf16[8,128,384]{2,1,0:T(8,128)(2,1)}, u32[]{:S(2)}, u32[]{:S(2)}) async-start(bf16[8,128,384]{2,1,0:T(8,128)(2,1)} %copy.165), calls=%async_computation.5 | async-start | bytes 1572864 | tf_op jit(solution)/shard_map/all_to_all | solution.py:116
  349.0 1.9 reshape.184
  350.9 2.6 multiply_reduce_fusion.1
  353.6 2.4 copy.170
  357.5 11.9 %all-to-all-done.5 = bf16[8,128,384]{2,1,0:T(8,128)(2,1)} async-done(((bf16[8,128,384]{2,1,0:T(8,128)(2,1)}), bf16[8,128,384]{2,1,0:T(8,128)(2,1)}, u32[]{:S(2)}, u32[]{:S(2)}) %all-to-all-start.5) | async-done | bytes 786464 | tf_op jit(solution)/shard_map/all_to_all | solution.py:116
  373.6 13.2 %all-reduce.2 = (f32[]{:T(128)}, f32[128]{0:T(128)S(1)}, f32[128]{0:T(128)S(1)}) all-reduce(f32[]{:T(128)} %fusion.51, f32[128]{0:T(128)S(1)} %multiply_reduce_fusion.1, f32[128]{0:T(128)S(1)} %get-tuple-element.303), channel_id=1, replica_groups=mesh['dp_0'=4,'dp_1'=4,'dp_2'=2,'seq'=8] {'dp_0'}, use_global_device_ids=true, to_apply=%region_14.15 | all-reduce | flops 257 | bytes 2056 | tf_op jit(solution)/shard_map/psum | solution.py:16
  386.9 11.0 %all-reduce.1 = (f32[]{:T(128)}, f32[128]{0:T(128)S(1)}, f32[128]{0:T(128)S(1)}) all-reduce(f32[]{:T(128)} %get-tuple-element.347, f32[128]{0:T(128)S(1)} %get-tuple-element.348, f32[128]{0:T(128)S(1)} %get-tuple-element.349), channel_id=1, replica_groups=mesh['dp_0'=4,'dp_1'=4,'dp_2'=2,'seq'=8] {'dp_1'}, use_global_device_ids=true, to_apply=%region_15.16 | all-reduce | flops 257 | bytes 2056 | tf_op jit(solution)/shard_map/psum | solution.py:16
  397.9 3.1 all-reduce.3
  401.0 16.2 %all-reduce = (f32[]{:T(128)}, f32[128]{0:T(128)S(1)}, f32[128]{0:T(128)S(1)}) all-reduce(f32[]{:T(128)} %get-tuple-element.350, f32[128]{0:T(128)S(1)} %get-tuple-element.351, f32[128]{0:T(128)S(1)} %get-tuple-element.352), channel_id=1, replica_groups=mesh['dp_0'=4,'dp_1'=4,'dp_2'=2,'seq'=8] {'seq'}, use_global_device_ids=true, to_apply=%region_17.18 | all-reduce | flops 257 | bytes 2056 | tf_op jit(solution)/shard_map/psum | solution.py:16
  (113 shorter events, 45.3 us)
Async XLA Ops:
  7.2 1.1 copy-start.12
  7.2 181.7 %all-gather.3.cloned.1.call-start = ((), (), s32[]{:S(2)}) async-start(), calls=%async_computation.8 | async-start | bytes 14155776 | tf_op jit(solution)/shard_map/all_gather | solution.py:75
  8.3 9.7 %copy-start.13 = (bf16[1,128,3072]{2,1,0:T(8,128)(2,1)S(1)}, bf16[1,128,3072]{2,1,0:T(8,128)(2,1)}, u32[]{:S(2)}) copy-start(bf16[1,128,3072]{2,1,0:T(8,128)(2,1)} %param.13) | copy-start | bytes 2359300
  9.5 35.9 %all-to-all-start = ((bf16[128,8,384]{0,2,1:T(8,128)(2,1)}), bf16[128,8,384]{0,2,1:T(8,128)(2,1)S(1)}, u32[]{:S(2)}, u32[]{:S(2)}) async-start(bf16[128,8,384]{0,2,1:T(8,128)(2,1)} %bitcast.4), calls=%async_computation | async-start | bytes 1572864 | tf_op jit(solution)/shard_map/all_to_all | solution.py:44
  18.0 33.2 %copy-start.14 = (bf16[1,128,3072]{2,1,0:T(8,128)(2,1)S(1)}, bf16[1,128,3072]{2,1,0:T(8,128)(2,1)}, u32[]{:S(2)}) copy-start(bf16[1,128,3072]{2,1,0:T(8,128)(2,1)} %param.14) | copy-start | bytes 2359300
  45.4 42.6 %copy-start.7 = (bf16[128,8,384]{0,2,1:T(8,128)(2,1)}, bf16[128,8,384]{0,2,1:T(8,128)(2,1)S(1)}, u32[]{:S(2)}) copy-start(bf16[128,8,384]{0,2,1:T(8,128)(2,1)S(1)} %all-to-all-done) | copy-start | bytes 2359300
  45.4 37.0 %all-to-all-start.1 = ((bf16[128,8,384]{0,2,1:T(8,128)(2,1)}), bf16[128,8,384]{0,2,1:T(8,128)(2,1)S(1)}, u32[]{:S(2)}, u32[]{:S(2)}) async-start(bf16[128,8,384]{0,2,1:T(8,128)(2,1)} %bitcast.8), calls=%async_computation.1 | async-start | bytes 1572864 | tf_op jit(solution)/shard_map/all_to_all | solution.py:45
  51.2 36.5 %copy-start.18 = (f32[128]{0:T(128)S(1)}, f32[128]{0:T(128)}, u32[]{:S(2)}) copy-start(f32[128]{0:T(128)} %param.18) | copy-start | bytes 1540
  51.2 36.5 %copy-start.19 = (s32[1,4]{1,0:T(1,128)S(1)}, s32[1,4]{1,0:T(1,128)}, u32[]{:S(2)}) copy-start(s32[1,4]{1,0:T(1,128)} %param.16) | copy-start | bytes 52
  82.4 5.6 %copy-start.11 = (bf16[128,8,384]{0,2,1:T(8,128)(2,1)}, bf16[128,8,384]{0,2,1:T(8,128)(2,1)S(1)}, u32[]{:S(2)}) copy-start(bf16[128,8,384]{0,2,1:T(8,128)(2,1)S(1)} %all-to-all-done.1) | copy-start | bytes 2359300
  82.4 36.3 %all-to-all-start.2 = ((bf16[128,8,384]{0,2,1:T(8,128)(2,1)}), bf16[128,8,384]{0,2,1:T(8,128)(2,1)}, u32[]{:S(2)}, u32[]{:S(2)}) async-start(bf16[128,8,384]{0,2,1:T(8,128)(2,1)} %bitcast.10), calls=%async_computation.2 | async-start | bytes 1572864 | tf_op jit(solution)/shard_map/all_to_all | solution.py:46
  87.7 284.4 %reduce-scatter.2.cloned.1.call-start = ((), (), s32[]{:S(2)}) async-start(), calls=%async_computation.7 | async-start | bytes 4866048 | tf_op jit(solution)/shard_map/reduce_scatter | solution.py:120
  89.0 1.7 copy-start.4
  95.6 0.7 copy-start.17
  125.7 1.9 copy-start.3
  130.5 3.5 copy-start
  134.0 1.9 copy-start.2
  134.0 1.9 copy-start.15
  135.9 2.6 copy-start.1
  138.5 0.9 copy-start.16
  141.1 3.5 copy-start
  144.5 1.9 copy-start.2
  144.5 1.9 copy-start.15
  146.5 2.6 copy-start.1
  149.1 0.9 copy-start.16
  289.5 28.7 %all-to-all-start.3 = ((bf16[8,128,384]{1,2,0:T(8,128)(2,1)}), bf16[8,128,384]{1,2,0:T(8,128)(2,1)}, u32[]{:S(2)}, u32[]{:S(2)}) async-start(bf16[8,128,384]{1,2,0:T(8,128)(2,1)} %fusion.47), calls=%async_computation.3 | async-start | bytes 1572864 | tf_op jit(solution)/shard_map/all_to_all | solution.py:110
  296.2 2.0 copy-start.8
  318.2 25.2 %all-to-all-start.4 = ((bf16[8,128,384]{2,1,0:T(8,128)(2,1)}), bf16[8,128,384]{2,1,0:T(8,128)(2,1)S(1)}, u32[]{:S(2)}, u32[]{:S(2)}) async-start(bf16[8,128,384]{2,1,0:T(8,128)(2,1)} %copy.163), calls=%async_computation.4 | async-start | bytes 1572864 | tf_op jit(solution)/shard_map/all_to_all | solution.py:113
  323.4 25.6 %copy-start.5 = (f32[8,128,384]{1,0,2:T(8,128)S(1)}, f32[8,128,384]{1,0,2:T(8,128)}, u32[]{:S(2)}) copy-start(f32[8,128,384]{1,0,2:T(8,128)} %copy-done.4) | copy-start | bytes 4718596
  343.4 5.5 %copy-start.9 = (bf16[8,128,384]{2,1,0:T(8,128)(2,1)}, bf16[8,128,384]{2,1,0:T(8,128)(2,1)S(1)}, u32[]{:S(2)}) copy-start(bf16[8,128,384]{2,1,0:T(8,128)(2,1)S(1)} %all-to-all-done.4) | copy-start | bytes 2359300
  343.4 25.9 %all-to-all-start.5 = ((bf16[8,128,384]{2,1,0:T(8,128)(2,1)}), bf16[8,128,384]{2,1,0:T(8,128)(2,1)}, u32[]{:S(2)}, u32[]{:S(2)}) async-start(bf16[8,128,384]{2,1,0:T(8,128)(2,1)} %copy.165), calls=%async_computation.5 | async-start | bytes 1572864 | tf_op jit(solution)/shard_map/all_to_all | solution.py:116
  349.0 1.9 copy-start.6
  353.6 2.4 copy-start.10
Sparse Core Ops, SparseCore 0:
  9.8 179.0 all-gather.2
  200.5 91.9 reduce-scatter.1
where the time goes:
time: 432 us; the launch traced here: 430 us
  waiting for transfers between devices  156 us (36%)
  matrix products  86.1 us (20%)
  local copies, waits for them, and re-layouts  60.2 us (14%)
  blocking collectives  43.5 us (10%)
  starting transfers between devices  36.9 us (9%)
  other arithmetic  26.9 us (6%)
  between operations  17.5 us (4%)
    psum x4, blocking collectives, one_axis_at_a_time(): array = lax.psum(array, axis)  43.5 us
    all_gather x1, waiting for transfers between devices, local(): out_full = lax.all_gather(out_grad[0], 'seq', axis=0, tiled=True)  32.1 us
    all_to_all x1, waiting for transfers between devices, local(): lax.all_to_all(key_rows[0], 'seq', split_axis=1, concat_axis=0, tiled=True)  30 us
    all_to_all x1, waiting for transfers between devices, local(): lax.all_to_all(query_rows[0], 'seq', split_axis=1, concat_axis=0, tiled=T...  26.2 us
    dot_general x2, matrix products, backward_block(): jnp.einsum('hqk,qhd->khd', d_scores, query_block, preferred_element_type=...  20.3 us
    all_to_all x1, waiting for transfers between devices, local(): lax.all_to_all(value_rows[0], 'seq', split_axis=1, concat_axis=0, tiled=T...  19.1 us
    dot_general x2, matrix products, backward_block(): jnp.einsum('hqk,khd->qhd', d_scores, k_norm, preferred_element_type=jnp.f...  19 us
    all_to_all x1, waiting for transfers between devices, local(): lax.all_to_all(key_grad.reshape(total, width), 'seq', split_axis=0, conca...  18.6 us
  transfers between devices with their start and end apart: 8, of which 7 were waited for; matrix products, arithmetic and copies ran while one was open for 35% of the time, Pallas kernels for 0%

commit v1 on v0

--- a/solution.py
+++ b/solution.py
@@ -42,7 +42,12 @@
 ):
     query, keys, values = (
         lax.all_to_all(query_rows[0], "seq", split_axis=1, concat_axis=0, tiled=True),
-        lax.all_to_all(key_rows[0], "seq", split_axis=1, concat_axis=0, tiled=True),
+        jnp.concatenate(
+            lax.all_to_all(
+                jnp.stack(jnp.split(key_rows[0], lax.axis_size("seq"), axis=1)), "seq", 0, 0
+            ),
+            axis=0,
+        ),
         lax.all_to_all(value_rows[0], "seq", split_axis=1, concat_axis=0, tiled=True),
     )
     total = query.shape[0]

time: 432 us -> 419 us (0.970)
  waiting for transfers between devices: 156 us -> 143 us
  local copies, waits for them, and re-layouts: 60.2 us -> 65.7 us
    all_to_all x1, waiting for transfers between devices: 18.6 us -> 3.09 us  [local(): lax.all_to_all(key_grad.reshape(total, width), 'seq', split_axis=0, conca...]
    unnamed x41 -> x43, local copies, waits for them, and re-layouts: 14.8 us -> 19.4 us
  transfers between devices with their start and end apart: 8 -> 8, of which waited for: 7 -> 7; matrix products, arithmetic and copies ran while one was open for 35% -> 37% of each run, Pallas kernels for 0% -> 0%
where the time goes in v1:
time: 419 us; the launch traced here: 418 us
  waiting for transfers between devices  143 us (34%)
  matrix products  85.8 us (20%)
  local copies, waits for them, and re-layouts  65.7 us (16%)
  blocking collectives  41.7 us (10%)
  starting transfers between devices  35.4 us (8%)
  other arithmetic  26.3 us (6%)
  between operations  17.5 us (4%)
    psum x4, blocking collectives, one_axis_at_a_time(): array = lax.psum(array, axis)  41.7 us
    all_gather x1, waiting for transfers between devices, local(): out_full = lax.all_gather(out_grad[0], 'seq', axis=0, tiled=True)  32 us
    all_to_all x1, waiting for transfers between devices, local(): lax.all_to_all(query_rows[0], 'seq', split_axis=1, concat_axis=0, tiled=T...  30 us
    all_to_all x1, waiting for transfers between devices, local(): lax.all_to_all(jnp.stack(jnp.split(key_rows[0], lax.axis_size('seq'), axi...  28.7 us
    dot_general x2, matrix products, backward_block(): jnp.einsum('hqk,qhd->khd', d_scores, query_block, preferred_element_type=...  20.1 us
    unnamed x43, local copies, waits for them, and re-layouts  19.4 us
    dot_general x2, matrix products, backward_block(): jnp.einsum('hqk,khd->qhd', d_scores, k_norm, preferred_element_type=jnp.f...  19 us
    all_to_all x1, waiting for transfers between devices, local(): lax.all_to_all(query_grad.reshape(total, width), 'seq', split_axis=0, con...  18.1 us
  transfers between devices with their start and end apart: 8, of which 7 were waited for; matrix products, arithmetic and copies ran while one was open for 37% of the time, Pallas kernels for 0%

profile of v1, /device:TPU:32, one launch (start us, length us, event | category | flops | bytes accessed | tf_op | source)
XLA Modules:
  0.0 418.0 jit_solution(7598361986365479915)
XLA Ops:
  13.5 8.6 %all-to-all-start.1 = ((bf16[8,128,384]{2,1,0:T(8,128)(2,1)}), bf16[8,128,384]{2,1,0:T(8,128)(2,1)S(1)}, u32[]{:S(2)}, u32[]{:S(2)}) async-start(bf16[8,128,384]{2,1,0:T(8,128)(2,1)} %fusion.52), calls=%async_computation.1 | async-start | bytes 1572864 | tf_op jit(solution)/shard_map/all_to_all | solution.py:46
  23.2 28.7 %all-to-all-done.1 = bf16[8,128,384]{2,1,0:T(8,128)(2,1)S(1)} async-done(((bf16[8,128,384]{2,1,0:T(8,128)(2,1)}), bf16[8,128,384]{2,1,0:T(8,128)(2,1)S(1)}, u32[]{:S(2)}, u32[]{:S(2)}) %all-to-all-start.1) | async-done | bytes 786464 | tf_op jit(solution)/shard_map/all_to_all | solution.py:46
  51.9 5.1 %all-to-all-start = ((bf16[128,8,384]{0,2,1:T(8,128)(2,1)}), bf16[128,8,384]{0,2,1:T(8,128)(2,1)S(1)}, u32[]{:S(2)}, u32[]{:S(2)}) async-start(bf16[128,8,384]{0,2,1:T(8,128)(2,1)} %bitcast.4), calls=%async_computation | async-start | bytes 1572864 | tf_op jit(solution)/shard_map/all_to_all | solution.py:44
  58.2 30.0 %all-to-all-done = bf16[128,8,384]{0,2,1:T(8,128)(2,1)S(1)} async-done(((bf16[128,8,384]{0,2,1:T(8,128)(2,1)}), bf16[128,8,384]{0,2,1:T(8,128)(2,1)S(1)}, u32[]{:S(2)}, u32[]{:S(2)}) %all-to-all-start) | async-done | bytes 786464 | tf_op jit(solution)/shard_map/all_to_all | solution.py:44
  88.2 5.3 %all-to-all-start.2 = ((bf16[128,8,384]{0,2,1:T(8,128)(2,1)}), bf16[128,8,384]{0,2,1:T(8,128)(2,1)}, u32[]{:S(2)}, u32[]{:S(2)}) async-start(bf16[128,8,384]{0,2,1:T(8,128)(2,1)} %bitcast.17), calls=%async_computation.2 | async-start | bytes 1572864 | tf_op jit(solution)/shard_map/all_to_all | solution.py:51
  98.7 2.3 copy.149
  102.3 2.1 copy.144
  104.3 2.6 reshape.176
  106.9 17.6 %all-to-all-done.2 = bf16[128,8,384]{0,2,1:T(8,128)(2,1)} async-done(((bf16[128,8,384]{0,2,1:T(8,128)(2,1)}), bf16[128,8,384]{0,2,1:T(8,128)(2,1)}, u32[]{:S(2)}, u32[]{:S(2)}) %all-to-all-start.2) | async-done | bytes 786464 | tf_op jit(solution)/shard_map/all_to_all | solution.py:51
  124.5 2.5 copy.147
  127.0 2.2 reshape.171
  129.2 2.3 copy.150
  134.6 21.1 %while.27 = (s32[]{:T(128)}, bf16[2,3,512,1024]{3,2,1,0:T(8,128)(2,1)}, bf16[2,512,3,128]{3,1,2,0:T(8,128)(2,1)}, s32[2]{0:T(128)S(1)}, s32[1024]{0:T(1024)S(1)}...) while((s32[]{:T(128)}, ...), condition=%wide.region_6.7_spmd, body=%wide.region_4.6_spmd.sunk | while | flops 817035776 | bytes 85746000 | solution.py:78
  136.3 3.4 fusion.83
  146.8 3.5 fusion.83
  155.7 3.1 copy.165
  158.8 2.2 copy.178
  160.9 32.0 %all-gather.3.cloned.1.call-done = bf16[1,1024,6144]{2,1,0:T(8,128)(2,1)} async-done(((bf16[1,128,6144]{2,1,0:T(8,128)(2,1)}), bf16[1,1024,6144]{2,1,0:T(8,128)(2,1)}) %all-gather.3.cloned.1.call-update) | async-done | bytes 12582928 | tf_op jit(solution)/shard_map/all_gather | solution.py:80
  192.9 11.4 %fusion.42 = bf16[384,6144]{0,1:T(8,128)(2,1)} fusion(bf16[1024,384]{0,1:T(8,128)(2,1)} %bitcast.199, bf16[1,1024,6144]{2,1,0:T(8,128)(2,1)} %all-gather.3.cloned.1.call-done), kind=kOutput, calls=%fused_computation.45 | convolution fusion | flops 4834197504 | bytes 18087936 | tf_op jit(solution)/shard_map/dot_general | solution.py:81
  204.3 10.4 %fusion.48 = bf16[1024,384]{0,1:T(8,128)(2,1)} fusion(bf16[384,6144]{1,0:T(8,128)(2,1)} %param.17, bf16[1,1024,6144]{2,1,0:T(8,128)(2,1)} %all-gather.3.cloned.1.call-done), kind=kOutput, calls=%fused_computation.61 | convolution fusion | flops 4832231424 | bytes 18087936 | tf_op jit(solution)/shard_map/dot_general | solution.py:82
  214.7 57.5 %while.28 = (s32[]{:T(128)}, f32[1024,3,128]{0,2,1:T(8,128)}, f32[1024,3,128]{0,2,1:T(8,128)S(1)}, f32[2,512,3,128]{3,1,2,0:T(8,128)}, s32[2]{0:T(128)S(1)}, /*i...) while((s32[]{:T(128)}, f32[1024,3,128]{0,2,1:T(8,128)}, ...), condition=%wide.region_9.10_spmd.clone, body=%wide.region_7.9_spmd.clone.sunk | while | flops 1634210816 | bytes 57019604 | solution.py:107
  216.0 5.0 %fusion.91 = f32[3,512,1024]{2,1,0:T(8,128)} fusion(bf16[1024,3,128]{2,0,1:T(8,128)(2,1)} %get-tuple-element.549, bf16[1024,3,128]{0,2,1:T(8,128)(2,1)} %get-tuple-element.548, s32[]{:T(128)S(6)} %select_n.24), kind=kOutput, calls=%fused_computation.30.clone.1 | convolution fusion | flops 402653184 | bytes 7471108 | tf_op jit(solution)/shard_map/while/body/eval_jaxpr/qhd,khd->hqk/dot_general | solution.py:93
  220.9 10.1 %bitcast_add_fusion.4 = f32[1024,3,128]{0,2,1:T(8,128)} fusion(f32[1024,3,128]{0,2,1:T(8,128)} %get-tuple-element.528, f32[3,512,1024]{2,1,0:T(8,128)} %fusion.91, bf16[2,3,512,1024]{3,2,1,0:T(8,128)(2,1)} %get-tuple-element.547, s32[]{:T(128)} %get-tuple-element.527, pred[]{:T(512)S(6)} %compare.3, bf16[1024,3,128]{0,2,1:T(8,128)(2,1)} %get-tuple-element.546, ...), kind=kOutput, calls=%fused_computation.26.clone.1 | convolution fusion | flops 414452224 | bytes 22414340 | tf_op jit(solution)/shard_map/while/body/eval_jaxpr/hqk,qhd->khd/dot_general | solution.py:100
  231.1 9.7 %fusion.92 = f32[2,512,3,128]{3,1,2,0:T(8,128)} fusion(f32[2,512,3,128]{3,1,2,0:T(8,128)} %get-tuple-element.530, s32[]{:T(128)} %get-tuple-element.527, bf16[1024,3,128]{2,0,1:T(8,128)(2,1)} %get-tuple-element.550, f32[3,512,1024]{2,1,0:T(8,128)} %fusion.91, bf16[2,3,512,1024]{3,2,1,0:T(8,128)(2,1)} %get-tuple-element.547), kind=kOutput, calls=%fused_computation.28.clone.1 | convolution fusion | flops 413665792 | bytes 20448768 | tf_op jit(solution)/shard_map/while/body/eval_jaxpr/hqk,khd->qhd/dot_general | solution.py:103
  240.7 3.0 bitcast_add_fusion.5
  245.0 4.9 %fusion.91 = f32[3,512,1024]{2,1,0:T(8,128)} fusion(bf16[1024,3,128]{2,0,1:T(8,128)(2,1)} %get-tuple-element.549, bf16[1024,3,128]{0,2,1:T(8,128)(2,1)} %get-tuple-element.548, s32[]{:T(128)S(6)} %select_n.24), kind=kOutput, calls=%fused_computation.30.clone.1 | convolution fusion | flops 402653184 | bytes 7471108 | tf_op jit(solution)/shard_map/while/body/eval_jaxpr/qhd,khd->hqk/dot_general | solution.py:93
  250.0 10.0 %bitcast_add_fusion.4 = f32[1024,3,128]{0,2,1:T(8,128)} fusion(f32[1024,3,128]{0,2,1:T(8,128)} %get-tuple-element.528, f32[3,512,1024]{2,1,0:T(8,128)} %fusion.91, bf16[2,3,512,1024]{3,2,1,0:T(8,128)(2,1)} %get-tuple-element.547, s32[]{:T(128)} %get-tuple-element.527, pred[]{:T(512)S(6)} %compare.3, bf16[1024,3,128]{0,2,1:T(8,128)(2,1)} %get-tuple-element.546, ...), kind=kOutput, calls=%fused_computation.26.clone.1 | convolution fusion | flops 414452224 | bytes 22414340 | tf_op jit(solution)/shard_map/while/body/eval_jaxpr/hqk,qhd->khd/dot_general | solution.py:100
  260.0 9.3 %fusion.92 = f32[2,512,3,128]{3,1,2,0:T(8,128)} fusion(f32[2,512,3,128]{3,1,2,0:T(8,128)} %get-tuple-element.530, s32[]{:T(128)} %get-tuple-element.527, bf16[1024,3,128]{2,0,1:T(8,128)(2,1)} %get-tuple-element.550, f32[3,512,1024]{2,1,0:T(8,128)} %fusion.91, bf16[2,3,512,1024]{3,2,1,0:T(8,128)(2,1)} %get-tuple-element.547), kind=kOutput, calls=%fused_computation.28.clone.1 | convolution fusion | flops 413665792 | bytes 20448768 | tf_op jit(solution)/shard_map/while/body/eval_jaxpr/hqk,khd->qhd/dot_general | solution.py:103
  269.3 2.9 bitcast_add_fusion.5
  272.3 2.0 multiply_reduce_fusion
  276.3 6.7 %all-to-all-start.4 = ((bf16[8,128,384]{2,1,0:T(8,128)(2,1)}), bf16[8,128,384]{2,1,0:T(8,128)(2,1)}, u32[]{:S(2)}, u32[]{:S(2)}) async-start(bf16[8,128,384]{2,1,0:T(8,128)(2,1)} %copy.161), calls=%async_computation.4 | async-start | bytes 1572864 | tf_op jit(solution)/shard_map/all_to_all | solution.py:118
  285.0 2.1 copy.154
  288.4 3.2 copy.158
  295.3 2.4 reshape.173
  297.7 4.3 %fusion.47 = bf16[8,128,384]{1,2,0:T(8,128)(2,1)} fusion(f32[8,128,384]{1,0,2:T(8,128)} %bitcast.183, f32[8,128,384]{1,0,2:T(8,128)} %reshape.173, f32[8,128,384]{1,0,2:T(8,128)} %bitcast.182, f32[384]{0:T(512)S(1)} %broadcast_bitcast_fusion, bf16[128,8,384]{0,2,1:T(8,128)(2,1)} %copy-done.7), kind=kLoop, calls=%fused_computation.49 | loop fusion | flops 2752512 | bytes 6292992 | tf_op jit(solution)/shard_map/convert_element_type | solution.py:37
  301.9 3.1 all-to-all-done.4
  305.0 4.2 all-to-all-start.3
  310.4 2.5 copy.163
  312.9 18.1 %all-to-all-done.3 = bf16[8,128,384]{1,2,0:T(8,128)(2,1)} async-done(((bf16[8,128,384]{1,2,0:T(8,128)(2,1)}), bf16[8,128,384]{1,2,0:T(8,128)(2,1)}, u32[]{:S(2)}, u32[]{:S(2)}) %all-to-all-start.3) | async-done | bytes 786464 | tf_op jit(solution)/shard_map/all_to_all | solution.py:115
  331.0 5.5 %all-to-all-start.5 = ((bf16[8,128,384]{2,1,0:T(8,128)(2,1)}), bf16[8,128,384]{2,1,0:T(8,128)(2,1)}, u32[]{:S(2)}, u32[]{:S(2)}) async-start(bf16[8,128,384]{2,1,0:T(8,128)(2,1)} %copy.163), calls=%async_computation.5 | async-start | bytes 1572864 | tf_op jit(solution)/shard_map/all_to_all | solution.py:121
  336.6 1.9 reshape.178
  338.5 2.6 multiply_reduce_fusion.1
  343.8 2.3 copy.168
  346.1 12.7 %all-to-all-done.5 = bf16[8,128,384]{2,1,0:T(8,128)(2,1)} async-done(((bf16[8,128,384]{2,1,0:T(8,128)(2,1)}), bf16[8,128,384]{2,1,0:T(8,128)(2,1)}, u32[]{:S(2)}, u32[]{:S(2)}) %all-to-all-start.5) | async-done | bytes 786464 | tf_op jit(solution)/shard_map/all_to_all | solution.py:121
  363.0 9.9 %all-reduce.2 = (f32[]{:T(128)}, f32[128]{0:T(128)S(1)}, f32[128]{0:T(128)S(1)}) all-reduce(f32[]{:T(128)} %fusion.51, f32[128]{0:T(128)S(1)} %multiply_reduce_fusion.1, f32[128]{0:T(128)S(1)} %get-tuple-element.303), channel_id=1, replica_groups=mesh['dp_0'=4,'dp_1'=4,'dp_2'=2,'seq'=8] {'dp_0'}, use_global_device_ids=true, to_apply=%region_14.15 | all-reduce | flops 257 | bytes 2056 | tf_op jit(solution)/shard_map/psum | solution.py:16
  372.9 12.5 %all-reduce.1 = (f32[]{:T(128)}, f32[128]{0:T(128)S(1)}, f32[128]{0:T(128)S(1)}) all-reduce(f32[]{:T(128)} %get-tuple-element.347, f32[128]{0:T(128)S(1)} %get-tuple-element.348, f32[128]{0:T(128)S(1)} %get-tuple-element.349), channel_id=1, replica_groups=mesh['dp_0'=4,'dp_1'=4,'dp_2'=2,'seq'=8] {'dp_1'}, use_global_device_ids=true, to_apply=%region_15.16 | all-reduce | flops 257 | bytes 2056 | tf_op jit(solution)/shard_map/psum | solution.py:16
  385.4 3.1 all-reduce.3
  388.5 16.2 %all-reduce = (f32[]{:T(128)}, f32[128]{0:T(128)S(1)}, f32[128]{0:T(128)S(1)}) all-reduce(f32[]{:T(128)} %get-tuple-element.350, f32[128]{0:T(128)S(1)} %get-tuple-element.351, f32[128]{0:T(128)S(1)} %get-tuple-element.352), channel_id=1, replica_groups=mesh['dp_0'=4,'dp_1'=4,'dp_2'=2,'seq'=8] {'seq'}, use_global_device_ids=true, to_apply=%region_17.18 | all-reduce | flops 257 | bytes 2056 | tf_op jit(solution)/shard_map/psum | solution.py:16
  (115 shorter events, 52.3 us)
Async XLA Ops:
  7.2 1.1 copy-start.10
  7.2 185.8 %all-gather.3.cloned.1.call-start = ((), (), s32[]{:S(2)}) async-start(), calls=%async_computation.8 | async-start | bytes 14155776 | tf_op jit(solution)/shard_map/all_gather | solution.py:80
  8.3 13.8 %copy-start.11 = (bf16[1,128,3072]{2,1,0:T(8,128)(2,1)S(1)}, bf16[1,128,3072]{2,1,0:T(8,128)(2,1)}, u32[]{:S(2)}) copy-start(bf16[1,128,3072]{2,1,0:T(8,128)(2,1)} %param.12) | copy-start | bytes 2359300
  13.5 38.4 %all-to-all-start.1 = ((bf16[8,128,384]{2,1,0:T(8,128)(2,1)}), bf16[8,128,384]{2,1,0:T(8,128)(2,1)S(1)}, u32[]{:S(2)}, u32[]{:S(2)}) async-start(bf16[8,128,384]{2,1,0:T(8,128)(2,1)} %fusion.52), calls=%async_computation.1 | async-start | bytes 1572864 | tf_op jit(solution)/shard_map/all_to_all | solution.py:46
  22.1 34.9 %copy-start.12 = (bf16[1,128,3072]{2,1,0:T(8,128)(2,1)S(1)}, bf16[1,128,3072]{2,1,0:T(8,128)(2,1)}, u32[]{:S(2)}) copy-start(bf16[1,128,3072]{2,1,0:T(8,128)(2,1)} %param.14) | copy-start | bytes 2359300
  51.9 36.3 %all-to-all-start = ((bf16[128,8,384]{0,2,1:T(8,128)(2,1)}), bf16[128,8,384]{0,2,1:T(8,128)(2,1)S(1)}, u32[]{:S(2)}, u32[]{:S(2)}) async-start(bf16[128,8,384]{0,2,1:T(8,128)(2,1)} %bitcast.4), calls=%async_computation | async-start | bytes 1572864 | tf_op jit(solution)/shard_map/all_to_all | solution.py:44
  57.0 36.5 %copy-start.17 = (s32[1,4]{1,0:T(1,128)S(1)}, s32[1,4]{1,0:T(1,128)}, u32[]{:S(2)}) copy-start(s32[1,4]{1,0:T(1,128)} %param.16) | copy-start | bytes 52
  88.2 5.3 %copy-start.7 = (bf16[128,8,384]{0,2,1:T(8,128)(2,1)}, bf16[128,8,384]{0,2,1:T(8,128)(2,1)S(1)}, u32[]{:S(2)}) copy-start(bf16[128,8,384]{0,2,1:T(8,128)(2,1)S(1)} %all-to-all-done) | copy-start | bytes 2359300
  88.2 36.3 %all-to-all-start.2 = ((bf16[128,8,384]{0,2,1:T(8,128)(2,1)}), bf16[128,8,384]{0,2,1:T(8,128)(2,1)}, u32[]{:S(2)}, u32[]{:S(2)}) async-start(bf16[128,8,384]{0,2,1:T(8,128)(2,1)} %bitcast.17), calls=%async_computation.2 | async-start | bytes 1572864 | tf_op jit(solution)/shard_map/all_to_all | solution.py:51
  93.5 268.0 %reduce-scatter.2.cloned.1.call-start = ((), (), s32[]{:S(2)}) async-start(), calls=%async_computation.7 | async-start | bytes 4866048 | tf_op jit(solution)/shard_map/reduce_scatter | solution.py:125
  96.9 0.7 copy-start.15
  129.2 4.0 copy-start.16
  131.6 1.9 copy-start.3
  136.3 3.4 copy-start
  139.7 1.9 copy-start.2
  139.7 1.9 copy-start.13
  141.7 2.6 copy-start.1
  144.3 0.9 copy-start.14
  146.8 3.5 copy-start
  150.3 1.9 copy-start.2
  150.3 1.9 copy-start.13
  152.2 2.6 copy-start.1
  154.8 0.9 copy-start.14
  272.2 2.1 copy-start.8
  276.3 28.7 %all-to-all-start.4 = ((bf16[8,128,384]{2,1,0:T(8,128)(2,1)}), bf16[8,128,384]{2,1,0:T(8,128)(2,1)}, u32[]{:S(2)}, u32[]{:S(2)}) async-start(bf16[8,128,384]{2,1,0:T(8,128)(2,1)} %copy.161), calls=%async_computation.4 | async-start | bytes 1572864 | tf_op jit(solution)/shard_map/all_to_all | solution.py:118
  283.3 1.8 copy-start.9
  288.4 3.2 copy-start.4
  293.5 1.7 copy-start.6
  305.0 26.0 %all-to-all-start.3 = ((bf16[8,128,384]{1,2,0:T(8,128)(2,1)}), bf16[8,128,384]{1,2,0:T(8,128)(2,1)}, u32[]{:S(2)}, u32[]{:S(2)}) async-start(bf16[8,128,384]{1,2,0:T(8,128)(2,1)} %fusion.47), calls=%async_computation.3 | async-start | bytes 1572864 | tf_op jit(solution)/shard_map/all_to_all | solution.py:115
  310.4 26.2 %copy-start.5 = (f32[8,128,384]{1,0,2:T(8,128)S(1)}, f32[8,128,384]{1,0,2:T(8,128)}, u32[]{:S(2)}) copy-start(f32[8,128,384]{1,0,2:T(8,128)} %copy.144) | copy-start | bytes 4718596
  331.0 27.8 %all-to-all-start.5 = ((bf16[8,128,384]{2,1,0:T(8,128)(2,1)}), bf16[8,128,384]{2,1,0:T(8,128)(2,1)}, u32[]{:S(2)}, u32[]{:S(2)}) async-start(bf16[8,128,384]{2,1,0:T(8,128)(2,1)} %copy.163), calls=%async_computation.5 | async-start | bytes 1572864 | tf_op jit(solution)/shard_map/all_to_all | solution.py:121
Sparse Core Ops, SparseCore 0:
  9.8 183.1 all-gather.2
  204.5 91.9 reduce-scatter.1
